TPU v7x, 256 devices: a whole 4x4x8 slice. The times are simulated.
256 devices in a mesh: owner: 8 (over x, core), rows: 32 (over z, y).
Axes of the slice: x: 4, y: 4, z: 8, core: 2. Of those that a mesh axis runs over, the one named last changes fastest.
Arguments:
- w_down: float32 [16, 6400, 4096], P('owner', None, 'rows'), may hold values from -0.15625 to 0.15625
- avg_down: bfloat16 [16, 6400, 4096], P('owner', None, 'rows'), may hold values from -0.0390625 to 0.0390625
- router_weight: float32 [4096, 16], P('rows', 'owner'), may hold values from -0.09375 to 0.09375
- router_gain: float32 [4096], P('rows'), may hold values from 0.25 to 1.75
Outputs:
- serve_down: bfloat16 [16, 6400, 4096], P('owner', 'rows')
- scale_down: float32 [16, 6400], P('owner', 'rows')
- serve_router: bfloat16 [4096, 16], replicated
All inputs are finite; a program needn't handle non-finite values. Where the computation divides by a largest or mean magnitude, that divisor is 1e-20 or more.
Results may differ from a plain program's by a relative error of at most 0.001.
Values may be sent and summed in bfloat16 or wider, within the bound.
No kernel may reach another device: no remote copies, remote signals or barrier semaphores. Data moves between devices by JAX's collectives and lax.ppermute only.
A program may use at most 64 MiB of HBM per device.

v0:
```python
import jax
import jax.numpy as jnp
from jax import lax
from jax.sharding import PartitionSpec as P

D_MODEL = 4096


def copy_for_each(x, axis):
    count = lax.axis_size(axis)
    return lax.all_to_all(jnp.broadcast_to(x[None], (count, *x.shape)), axis, 0, 0, tiled=True)


def over_copies(x, axis):
    everything = copy_for_each(x, axis)
    return jnp.sum(everything, axis=0)


def laid_out(parts, dim):
    shape = list(parts.shape[1:])
    shape[dim] *= parts.shape[0]
    return jnp.moveaxis(parts, 0, dim).reshape(shape)


def collect(x, axis, dim):
    return laid_out(copy_for_each(x, axis), dim)


def per_device(w_down, avg_down, router_weight, router_gain):
    fresh_down = w_down + avg_down.astype(jnp.float32)
    total_down = over_copies(jnp.sum(jnp.abs(fresh_down), axis=2), "rows")
    scale_down = total_down / D_MODEL
    narrow_down = (fresh_down / jnp.expand_dims(scale_down, 2)).astype(jnp.bfloat16)
    serve_down = lax.all_to_all(narrow_down, "rows", split_axis=1, concat_axis=2, tiled=True)
    scale_down = lax.dynamic_slice_in_dim(
        scale_down, lax.axis_index("rows") * serve_down.shape[1], serve_down.shape[1], axis=1
    )
    part_router = (router_weight * router_gain[:, None]).astype(jnp.bfloat16)
    row_router = collect(part_router, "rows", 0)
    serve_router = collect(row_router, "owner", 1)
    return (serve_down, scale_down, serve_router)


def solution(mesh):
    return jax.shard_map(
        per_device,
        mesh=mesh,
        in_specs=(
            P("owner", None, "rows"),
            P("owner", None, "rows"),
            P("rows", "owner"),
            P("rows"),
        ),
        out_specs=(P("owner", "rows", None), P("owner", "rows"), P()),
        check_vma=False,
    )
```

profile of v0, /device:TPU:9, one launch (start us, length us, event | category | flops | bytes accessed | tf_op | source)
XLA Modules:
  0.0 201.1 jit_solution(2779808520759683975)
XLA Ops:
  0.6 0.7 multiply_convert_fusion
  1.3 0.6 broadcast_in_dim.9
  1.9 11.1 %all-to-all-start.2 = ((bf16[32,128,2]{1,2,0:T(2,128)(2,1)}), bf16[32,128,2]{1,2,0:T(2,128)(2,1)S(1)}, u32[]{:S(2)}, u32[]{:S(2)}) async-start(bf16[32,128,2]{1,2,0:T(2,128)(2,1)} %broadcast_in_dim.9), calls=%async_computation.2 | async-start | bytes 32768 | tf_op jit(solution)/shard_map/all_to_all | solution.py:11
  13.1 5.6 %abs_reduce_fusion = f32[2,6400]{1,0:T(2,128)S(1)} fusion(f32[2,6400,128]{2,1,0:T(8,128)} %param.4, bf16[2,6400,128]{2,1,0:T(8,128)(2,1)} %param.5), kind=kLoop, calls=%fused_computation.1 | loop fusion | flops 6540800 | bytes 9881600 | tf_op jit(solution)/shard_map/reduce_sum | solution.py:31
  18.7 0.0 copy-start
  18.7 2.0 all-to-all-done.2
  20.7 0.4 broadcast_in_dim.8
  21.1 46.8 %all_to_all.33 = f32[32,2,6400]{2,1,0:T(2,128)} all-to-all(f32[32,2,6400]{2,1,0:T(2,128)S(1)} %broadcast_in_dim.8), channel_id=1, replica_groups=mesh['owner'=8,'rows'=32] {'rows'}, dimensions={0} | all-to-all | bytes 3276800 | tf_op jit(solution)/shard_map/all_to_all | solution.py:11
  67.9 0.7 broadcast_in_dim.11
  68.6 6.7 %all-to-all-start.3 = ((bf16[8,4096,2]{1,2,0:T(2,128)(2,1)}), bf16[8,4096,2]{1,2,0:T(2,128)(2,1)S(1)}, u32[]{:S(2)}, u32[]{:S(2)}) async-start(bf16[8,4096,2]{1,2,0:T(2,128)(2,1)} %broadcast_in_dim.11), calls=%async_computation.3 | async-start | bytes 262144 | tf_op jit(solution)/shard_map/all_to_all | solution.py:11
  75.4 1.9 reduce_sum.19
  77.3 0.0 copy-done
  77.3 4.7 %divide_convert_fusion = bf16[2,6400,128]{2,1,0:T(8,128)(2,1)S(1)} fusion(f32[2,6400,128]{2,1,0:T(8,128)} %param.4, bf16[2,6400,128]{2,1,0:T(8,128)(2,1)S(1)} %copy-done, f32[2,6400]{1,0:T(2,128)S(1)} %broadcast_multiply_fusion), kind=kLoop, calls=%fused_computation | loop fusion | flops 6553600 | bytes 13158400 | tf_op jit(solution)/shard_map/convert_element_type | solution.py:33
  82.0 27.9 %copy.31 = bf16[2,6400,128]{2,0,1:T(2,128)(2,1)} copy(bf16[2,6400,128]{2,1,0:T(8,128)(2,1)S(1)} %divide_convert_fusion) | data formatting | bytes 6553600 | tf_op jit(solution)/shard_map/convert_element_type | solution.py:33
  109.9 0.0 all-to-all-done.3
  109.9 5.0 %all-to-all-start.1 = ((bf16[2,6400,128]{2,0,1:T(2,128)(2,1)}), bf16[2,6400,128]{2,0,1:T(2,128)(2,1)S(1)}, u32[]{:S(2)}, u32[]{:S(2)}) async-start(bf16[2,6400,128]{2,0,1:T(2,128)(2,1)} %copy.31), calls=%async_computation.1 | async-start | bytes 6553600 | tf_op jit(solution)/shard_map/all_to_all | solution.py:34
  114.9 0.7 reshape.16
  115.7 0.7 constant_dynamic-slice_fusion
  116.3 76.1 %all-to-all-done.1 = bf16[2,6400,128]{2,0,1:T(2,128)(2,1)S(1)} async-done(((bf16[2,6400,128]{2,0,1:T(2,128)(2,1)}), bf16[2,6400,128]{2,0,1:T(2,128)(2,1)S(1)}, u32[]{:S(2)}, u32[]{:S(2)}) %all-to-all-start.1) | async-done | bytes 3276832 | tf_op jit(solution)/shard_map/all_to_all | solution.py:34
  192.4 2.5 %copy.32 = bf16[2,200,32,128]{3,2,1,0:T(8,128)(2,1)} copy(bf16[2,200,32,128]{3,0,1,2:T(2,128)(2,1)S(1)} %bitcast.9) | data formatting | bytes 6553600 | tf_op jit(solution)/shard_map/all_to_all | solution.py:34
  194.9 6.2 %all_to_all.26 = bf16[2,200,4096]{2,1,0:T(8,128)(2,1)} reshape(bf16[2,200,32,128]{3,2,1,0:T(8,128)(2,1)} %copy.32) | data formatting | bytes 6553600 | tf_op jit(solution)/shard_map/all_to_all | solution.py:34
  (1 shorter events, 0.0 us)
Async XLA Ops:
  1.9 18.8 %all-to-all-start.2 = ((bf16[32,128,2]{1,2,0:T(2,128)(2,1)}), bf16[32,128,2]{1,2,0:T(2,128)(2,1)S(1)}, u32[]{:S(2)}, u32[]{:S(2)}) async-start(bf16[32,128,2]{1,2,0:T(2,128)(2,1)} %broadcast_in_dim.9), calls=%async_computation.2 | async-start | bytes 32768 | tf_op jit(solution)/shard_map/all_to_all | solution.py:11
  18.7 58.6 %copy-start = (bf16[2,6400,128]{2,1,0:T(8,128)(2,1)S(1)}, bf16[2,6400,128]{2,1,0:T(8,128)(2,1)}, u32[]{:S(2)}) copy-start(bf16[2,6400,128]{2,1,0:T(8,128)(2,1)} %param.5) | copy-start | bytes 9830404
  68.6 41.3 %all-to-all-start.3 = ((bf16[8,4096,2]{1,2,0:T(2,128)(2,1)}), bf16[8,4096,2]{1,2,0:T(2,128)(2,1)S(1)}, u32[]{:S(2)}, u32[]{:S(2)}) async-start(bf16[8,4096,2]{1,2,0:T(2,128)(2,1)} %broadcast_in_dim.11), calls=%async_computation.3 | async-start | bytes 262144 | tf_op jit(solution)/shard_map/all_to_all | solution.py:11
  109.9 82.5 %all-to-all-start.1 = ((bf16[2,6400,128]{2,0,1:T(2,128)(2,1)}), bf16[2,6400,128]{2,0,1:T(2,128)(2,1)S(1)}, u32[]{:S(2)}, u32[]{:S(2)}) async-start(bf16[2,6400,128]{2,0,1:T(2,128)(2,1)} %copy.31), calls=%async_computation.1 | async-start | bytes 6553600 | tf_op jit(solution)/shard_map/all_to_all | solution.py:34
where the time goes:
time: 202 us; the launch traced here: 201 us
  waiting for transfers between devices  78.1 us (39%)
  blocking collectives  46.8 us (23%)
  local copies, waits for them, and re-layouts  39.7 us (20%)
  starting transfers between devices  22.9 us (11%)
  other arithmetic  12.9 us (6%)
    all_to_all x1, waiting for transfers between devices, per_device(): lax.all_to_all(narrow_down, 'rows', split_axis=1, concat_axis=2, tiled=True)  76.1 us
    all_to_all x1, blocking collectives, copy_for_each(): lax.all_to_all(jnp.broadcast_to(x[None], (count, *x.shape)), axis, 0, 0,...  46.8 us
    convert_element_type x1, local copies, waits for them, and re-layouts, per_device(): (fresh_down / jnp.expand_dims(scale_down, 2)).astype(jnp.bfloat16)  27.9 us
    all_to_all x2, starting transfers between devices, copy_for_each(): lax.all_to_all(jnp.broadcast_to(x[None], (count, *x.shape)), axis, 0, 0,...  17.8 us
    all_to_all x2, local copies, waits for them, and re-layouts, per_device(): lax.all_to_all(narrow_down, 'rows', split_axis=1, concat_axis=2, tiled=True)  8.72 us
    reduce_sum x1, other arithmetic, per_device(): total_down = over_copies(jnp.sum(jnp.abs(fresh_down), axis=2), 'rows')  5.6 us
    all_to_all x1, starting transfers between devices, per_device(): lax.all_to_all(narrow_down, 'rows', split_axis=1, concat_axis=2, tiled=True)  5.01 us
    convert_element_type x1, other arithmetic, per_device(): (fresh_down / jnp.expand_dims(scale_down, 2)).astype(jnp.bfloat16)  4.74 us
  transfers between devices with their start and end apart: 3, of which 2 were waited for; matrix products, arithmetic and copies ran while one was open for 21% of the time, Pallas kernels for 0%

commit v1 on v0

v1 whole, which is shorter than its diff:
```python
import jax
import jax.numpy as jnp
from jax import lax
from jax.experimental import pallas as pl
from jax.experimental.pallas import tpu as pltpu
from jax.sharding import PartitionSpec as P

D_MODEL = 4096
LANES = 128
STEP = 40
BITS = 10
FINE = 8.0
SPAN = 239.0
MID = 120.0
ROOM = 24 * 2**20


def lane_of(shape):
    return lax.broadcasted_iota(jnp.int32, shape, len(shape) - 1)


def encode_kernel(w_ref, a_ref, o_ref):
    fresh = w_ref[...] + a_ref[...].astype(jnp.float32)
    size = jnp.abs(fresh)
    top = jnp.max(size, axis=-1, keepdims=True)
    level = jnp.clip(jnp.floor(FINE * (-2.0 - jnp.log2(top))), 0.0, 880.0)
    place = size * (jnp.exp2(2.0 + level * (1.0 / FINE)) * SPAN)
    lane = lane_of((1, 1, 1, LANES))
    digit = jnp.floor(level * jnp.exp2(-jnp.minimum(lane, BITS).astype(jnp.float32)))
    digit = digit - 2.0 * jnp.floor(digit * 0.5)
    marked = jnp.floor(place * 32.0 + 0.5) * (1.0 / 32.0) + digit * (1.0 / 64.0)
    place = jnp.where(lane < BITS, marked, place)
    code = jnp.exp2(place - MID)
    o_ref[...] = jnp.swapaxes(jnp.where(fresh < 0.0, -code, code).astype(jnp.bfloat16), 0, 1)


def encode(w, a):
    experts, count, rows, width = w.shape
    group = 2
    spec = pl.BlockSpec((experts, group, rows, width), lambda d: (0, d, 0, 0))
    return pl.pallas_call(
        encode_kernel,
        grid=(count // group,),
        in_specs=[spec, spec],
        out_specs=pl.BlockSpec((group, experts, rows, width), lambda d: (d, 0, 0, 0)),
        out_shape=jax.ShapeDtypeStruct((count, experts, rows, width), jnp.bfloat16),
        cost_estimate=pl.CostEstimate(flops=w.size * 30, transcendentals=0, bytes_accessed=w.size * 8),
        name="encode",
    )(w, a)


def decode_kernel(c_ref, d_ref, s_ref):
    count, _, rows, _ = c_ref.shape
    expert, step = pl.program_id(0), pl.program_id(1)
    lane = lane_of((1, 1, LANES))
    weight = jnp.where(lane < BITS, jnp.exp2(lane.astype(jnp.float32)), 0.0)
    wide = lax.broadcasted_iota(jnp.int32, (8, 256), 1)
    row = lax.broadcasted_iota(jnp.int32, (8, 256), 0)
    spread = jnp.zeros((8, 256), jnp.float32)
    for r in range(0, STEP, 8):
        start = pl.multiple_of(step * STEP + r, 8)
        code = c_ref[:, expert, pl.ds(start, 8), :].astype(jnp.float32)
        place = jnp.log2(jnp.abs(code)) + MID
        units = jnp.floor(place * 64.0 + 0.5)
        half = jnp.floor(units * 0.5)
        level = jnp.sum((units - 2.0 * half) * weight, axis=-1, keepdims=True)
        place = jnp.where(lane < BITS, half * (1.0 / 32.0), place)
        size = place * (jnp.exp2(-2.0 - level * (1.0 / FINE)) * (1.0 / SPAN))
        scale = jnp.sum(jnp.sum(size, axis=0), axis=-1, keepdims=True) * (1.0 / D_MODEL)
        value = jnp.where(code < 0.0, -size, size) / scale
        value = value.astype(jnp.bfloat16)
        for s in range(count):
            d_ref[0, r : r + 8, s * LANES : (s + 1) * LANES] = value[s]
        spread = jnp.where(wide == row + start, scale, spread)
    line = jnp.sum(spread, axis=0, keepdims=True)[:, :rows]
    here = lax.broadcasted_iota(jnp.int32, s_ref.shape, 1) - step * STEP
    mine = lax.broadcasted_iota(jnp.int32, s_ref.shape, 0) == expert
    s_ref[...] = jnp.where(mine & (here >= 0) & (here < STEP), line, s_ref[...])


def decode(code):
    count, experts, rows, width = code.shape
    return pl.pallas_call(
        decode_kernel,
        grid=(experts, rows // STEP),
        in_specs=[pl.BlockSpec(memory_space=pltpu.VMEM)],
        out_specs=[
            pl.BlockSpec((1, STEP, count * width), lambda e, r: (e, r, 0)),
            pl.BlockSpec((experts, rows), lambda e, r: (0, 0)),
        ],
        out_shape=[
            jax.ShapeDtypeStruct((experts, rows, count * width), jnp.bfloat16),
            jax.ShapeDtypeStruct((experts, rows), jnp.float32),
        ],
        cost_estimate=pl.CostEstimate(flops=code.size * 30, transcendentals=0, bytes_accessed=code.size * 4),
        compiler_params=pltpu.CompilerParams(vmem_limit_bytes=ROOM),
        name="decode",
    )(code)


def per_device(w_down, avg_down, router_weight, router_gain):
    experts, inner, width = w_down.shape
    count = lax.axis_size("rows")
    blocks = (experts, count, inner // count, width)
    code = lax.all_to_all(encode(w_down.reshape(blocks), avg_down.reshape(blocks)), "rows", 0, 0, tiled=True)
    serve, scale = decode(code)

    part = (router_weight * router_gain[:, None]).astype(jnp.bfloat16).T
    router = lax.all_gather(part, ("owner", "rows"), axis=0)
    router = router.reshape(-1, count, *part.shape).transpose(1, 3, 0, 2)
    return serve, scale, router.reshape(D_MODEL, -1)


def solution(mesh):
    return jax.shard_map(
        per_device,
        mesh=mesh,
        in_specs=(
            P("owner", None, "rows"),
            P("owner", None, "rows"),
            P("rows", "owner"),
            P("rows"),
        ),
        out_specs=(P("owner", "rows", None), P("owner", "rows"), P()),
        check_vma=False,
    )
```

time: 202 us -> 156 us (0.77)
  waiting for transfers between devices: 78.1 us -> 0.01 us
  blocking collectives: 46.8 us -> 119 us
  local copies, waits for them, and re-layouts: 39.7 us -> 0.74 us
  Pallas kernels: 0 us -> 21.8 us
  other arithmetic: 12.9 us -> 0.01 us
  starting transfers between devices: 22.9 us -> 11.3 us
    all_gather x0 -> x1, blocking collectives: none -> 119 us  [per_device(): router = lax.all_gather(part, ('owner', 'rows'), axis=0)]
    all_to_all x3 -> x1, waiting for transfers between devices: 78.1 us -> 0.01 us  [per_device(): lax.all_to_all(encode(w_down.reshape(blocks), avg_down.reshape(blocks)),...]
    all_to_all x1 -> x0, blocking collectives: 46.8 us -> none  [copy_for_each(): lax.all_to_all(jnp.broadcast_to(x[None], (count, *x.shape)), axis, 0, 0,...]
    convert_element_type x1 -> x0, local copies, waits for them, and re-layouts: 27.9 us -> none  [per_device(): (fresh_down / jnp.expand_dims(scale_down, 2)).astype(jnp.bfloat16)]
    pallas_call x0 -> x2, Pallas kernels: none -> 21.8 us  [the longest x1 14.6 us: encode(): pl.pallas_call(encode_kernel, grid=(count // group,), in_specs=[spec, spe...]
    all_to_all x3 -> x1, starting transfers between devices: 22.9 us -> 11.3 us  [per_device(): lax.all_to_all(encode(w_down.reshape(blocks), avg_down.reshape(blocks)),...]
    all_to_all x2 -> x0, local copies, waits for them, and re-layouts: 8.72 us -> none  [per_device(): lax.all_to_all(narrow_down, 'rows', split_axis=1, concat_axis=2, tiled=True)]
    reduce_sum x2 -> x0, other arithmetic: 7.5 us -> none  [the longest x1 5.6 us: per_device(): total_down = over_copies(jnp.sum(jnp.abs(fresh_down), axis=2), 'rows')]
  transfers between devices with their start and end apart: 3 -> 1, of which waited for: 2 -> 0; matrix products, arithmetic and copies ran while one was open for 21% -> 0% of each run, Pallas kernels for 0% -> 0%
where the time goes in v1:
time: 156 us; the launch traced here: 154 us
  blocking collectives  119 us (76%)
  Pallas kernels  21.8 us (14%)
  starting transfers between devices  11.3 us (7%)
    all_gather x1, blocking collectives, per_device(): router = lax.all_gather(part, ('owner', 'rows'), axis=0)  119 us
    pallas_call x1, Pallas kernels, encode(): pl.pallas_call(encode_kernel, grid=(count // group,), in_specs=[spec, spe...  14.6 us
    all_to_all x1, starting transfers between devices, per_device(): lax.all_to_all(encode(w_down.reshape(blocks), avg_down.reshape(blocks)),...  11.3 us
    pallas_call x1, Pallas kernels, decode(): pl.pallas_call(decode_kernel, grid=(experts, rows // STEP), in_specs=[pl....  7.26 us
  transfers between devices with their start and end apart: 1, of which 0 were waited for; matrix products, arithmetic and copies ran while one was open for 0% of the time, Pallas kernels for 0%

profile of v1, /device:TPU:9, one launch (start us, length us, event | category | flops | bytes accessed | tf_op | source)
XLA Modules:
  0.0 153.9 jit_solution(7018776082660959187)
XLA Ops:
  0.6 14.6 %encode.1 = bf16[32,2,200,128]{3,2,1,0:T(8,128)(2,1)} custom-call(f32[2,32,200,128]{3,2,1,0:T(8,128)} %bitcast.16, bf16[2,32,200,128]{3,2,1,0:T(8,128)(2,1)} %bitcast.17), custom_call_target="tpu_custom_call" | custom-call | flops 49152000 | bytes 13107200 | tf_op jit(solution)/shard_map/encode/pallas_call | solution.py:41
  15.2 0.0 copy-start
  15.2 0.0 copy-start.1
  15.2 11.3 %all-to-all-start = ((bf16[32,2,200,128]{3,2,1,0:T(8,128)(2,1)}), bf16[32,2,200,128]{3,2,1,0:T(8,128)(2,1)S(1)}, u32[]{:S(2)}, u32[]{:S(2)}) async-start(bf16[32,2,200,128]{3,2,1,0:T(8,128)(2,1)} %encode.1), calls=%async_computation | async-start | bytes 6553600 | tf_op jit(solution)/shard_map/all_to_all | solution.py:105
  26.5 0.0 copy-done
  26.5 0.0 copy-done.1
  26.5 119.4 %all-gather.1 = bf16[256,2,128]{2,1,0:T(2,128)(2,1)S(1)} all-gather(bf16[1,2,128]{2,1,0:T(2,128)(2,1)S(1)} %fusion), channel_id=2, replica_groups=mesh['owner'=8,'rows'=32] {'owner','rows'}, dimensions={0}, use_global_device_ids=true | all-gather | bytes 131584 | tf_op jit(solution)/shard_map/all_gather | solution.py:109
  145.9 0.7 copy.11
  146.6 0.0 all-to-all-done.c_ref
  146.6 7.3 %decode.1 = (bf16[2,200,4096]{2,1,0:T(8,128)(2,1)}, f32[2,200]{1,0:T(2,128)}) custom-call(bf16[32,2,200,128]{3,2,1,0:T(8,128)(2,1)S(1)} %all-to-all-done.c_ref), custom_call_target="tpu_custom_call" | custom-call | flops 49152000 | bytes 6553600 | tf_op jit(solution)/shard_map/decode/pallas_call | solution.py:83
  (2 shorter events, 0.0 us)
Async XLA Ops:
  15.2 11.3 %copy-start = (f32[128,2]{0,1:T(2,128)S(1)}, f32[128,2]{0,1:T(2,128)}, u32[]{:S(2)}) copy-start(f32[128,2]{0,1:T(2,128)} %param.6) | copy-start | bytes 3076
  15.2 11.3 %copy-start.1 = (f32[128]{0:T(128)S(1)}, f32[128]{0:T(128)}, u32[]{:S(2)}) copy-start(f32[128]{0:T(128)} %param.7) | copy-start | bytes 1540
  15.2 131.4 %all-to-all-start = ((bf16[32,2,200,128]{3,2,1,0:T(8,128)(2,1)}), bf16[32,2,200,128]{3,2,1,0:T(8,128)(2,1)S(1)}, u32[]{:S(2)}, u32[]{:S(2)}) async-start(bf16[32,2,200,128]{3,2,1,0:T(8,128)(2,1)} %encode.1), calls=%async_computation | async-start | bytes 6553600 | tf_op jit(solution)/shard_map/all_to_all | solution.py:105
